TPU v7x, 32 devices: a whole 2x2x4 slice. The times are simulated.
32 devices in a mesh: fsdp: 8 (over z, y), dp: 4 (over x, core).
Axes of the slice: x: 2, y: 2, z: 4, core: 2. Of those that a mesh axis runs over, the one named last changes fastest.
Arguments:
- tokens: bfloat16 [512, 4096], P('dp', 'fsdp'), may hold values from -6 to 6
- out_grad: bfloat16 [512, 5120], P('dp', 'fsdp'), may hold values from -0.26367188 to 0.26367188
- master: float32 [4096, 5120], P('fsdp'), may hold values from -0.09375 to 0.09375
- moment_one: float32 [4096, 5120], P('fsdp'), may hold values from -3 to 3
- moment_two: float32 [4096, 5120], P('fsdp'), may hold values from 0.1 to 4
- flags: int32 [32, 16], P(('fsdp', 'dp')), may hold values 0 or 1
- steps: int32 [16], replicated, may hold values from 1 to 8
- rate: float32 [1], replicated, may hold values from 0.001 to 0.01
Outputs:
- master_next: float32 [4096, 5120], P('fsdp')
- moment_one_next: float32 [4096, 5120], P('fsdp')
- moment_two_next: float32 [4096, 5120], P('fsdp')
- weight_half: bfloat16 [4096, 5120], P('fsdp')
- steps_next: int32 [16], replicated
- outputs: bfloat16 [512, 5120], P('dp', 'fsdp')
All inputs are finite; a program needn't handle non-finite values. No bound on the sum of `flags` on one device may be relied on, other than what follows from the above.
Results may differ from a plain program's by a relative error of at most 0.0049.
Values may be sent and summed in bfloat16 or wider, within the bound.
A program may use at most 128 MiB of HBM per device.

v0:
```python
import jax
import jax.numpy as jnp
from jax import lax
from jax.sharding import PartitionSpec as P

BUCKETS = 16


first_decay = 0.9
second_decay = 0.95
epsilon = 1e-08


def local(tokens, out_grad, master, moment_one, moment_two, flags, steps, rate):
    width_out = master.shape[1]
    bucket_width = width_out // BUCKETS
    contract_rows = (((0,), (0,)), ((), ()))
    gathered, flag_rows = (
        lax.all_gather(out_grad, "fsdp", axis=1, tiled=True),
        lax.all_gather(flags.astype(jnp.bfloat16), "fsdp", axis=0, tiled=True),
    )
    partial_value = lax.dot_general(
        tokens, gathered, contract_rows, preferred_element_type=jnp.float32
    )
    local_counts = jnp.sum(flag_rows.astype(jnp.float32), axis=0)
    gradient, counts = lax.psum((partial_value, local_counts), "dp")
    commit_bucket = counts == 0.0
    commit = jnp.repeat(commit_bucket, bucket_width)[None, :]
    times = jnp.repeat(steps + 1, bucket_width).astype(jnp.float32)[None, :]
    first = first_decay * moment_one + (1.0 - first_decay) * gradient
    second = second_decay * moment_two + (1.0 - second_decay) * gradient * gradient
    fix_one = 1.0 - jnp.power(jnp.float32(first_decay), times)
    fix_two = 1.0 - jnp.power(jnp.float32(second_decay), times)
    candidate = master - rate[0] * (first / fix_one) / (jnp.sqrt(second / fix_two) + epsilon)
    master_next = jnp.where(commit, candidate, master)
    moment_one_next = jnp.where(commit, first, moment_one)
    moment_two_next = jnp.where(commit, second, moment_two)
    weight_half = master_next.astype(jnp.bfloat16)
    steps_next = steps + commit_bucket.astype(jnp.int32)
    result = lax.psum_scatter(
        lax.dot_general(
            weight_half, tokens, (((0,), (1,)), ((), ())), preferred_element_type=jnp.float32
        ),
        "fsdp",
        scatter_dimension=0,
        tiled=True,
    ).T
    return (
        master_next,
        moment_one_next,
        moment_two_next,
        weight_half,
        steps_next,
        result.astype(jnp.bfloat16),
    )


def solution(mesh):
    in_specs = (
        P("dp", "fsdp"),
        P("dp", "fsdp"),
        P("fsdp", None),
        P("fsdp", None),
        P("fsdp", None),
        P(("fsdp", "dp"), None),
        P(),
        P(),
    )
    out_specs = (
        P("fsdp", None),
        P("fsdp", None),
        P("fsdp", None),
        P("fsdp", None),
        P(),
        P("dp", "fsdp"),
    )
    return jax.shard_map(local, mesh=mesh, in_specs=in_specs, out_specs=out_specs, check_vma=False)
```

profile of v0, /device:TPU:0, one launch (start us, length us, event | category | flops | bytes accessed | tf_op | source)
XLA Modules:
  0.0 359.2 jit_solution(1873020660549578413)
XLA Ops:
  7.2 0.0 copy-start
  7.2 0.0 all-gather.3.cloned.1.call-start
  7.2 0.7 all-gather.3.cloned.1.call-update
  7.9 0.0 copy-start.2
  7.9 0.0 copy-start.3
  7.9 0.0 all-reduce.2.cloned.1.call-start
  8.0 47.5 %all-gather.3.cloned.1.call-done = bf16[128,5120]{1,0:T(8,128)(2,1)} async-done(((bf16[128,640]{1,0:T(8,128)(2,1)}), bf16[128,5120]{1,0:T(8,128)(2,1)}) %all-gather.3.cloned.1.call-update) | async-done | bytes 1310736 | tf_op jit(solution)/shard_map/all_gather | solution.py:19
  55.5 0.0 copy-done
  55.5 7.0 %fusion.4 = f32[512,5120]{1,0:T(8,128)} fusion(bf16[128,512]{1,0:T(8,128)(2,1)S(1)} %copy-done, bf16[128,5120]{1,0:T(8,128)(2,1)} %all-gather.3.cloned.1.call-done), kind=kOutput, calls=%fused_computation.14 | convolution fusion | flops 671088640 | bytes 11927552 | tf_op jit(solution)/shard_map/dot_general | solution.py:22
  62.5 0.0 all-reduce.2.cloned.1.call-update
  62.5 0.0 reduce-scatter.2.cloned.1.call-start
  63.2 0.0 copy-done.2
  63.2 18.1 %all-gather = bf16[8,1,16]{2,1,0:T(2,128)(2,1)S(1)} all-gather(bf16[1,1,16]{2,1,0:T(2,128)(2,1)S(1)} %convert_bitcast_fusion.1), channel_id=1, replica_groups=mesh['fsdp'=8,'dp'=4] {'fsdp'}, dimensions={0}, use_global_device_ids=true | all-gather | bytes 288 | tf_op jit(solution)/shard_map/all_gather | solution.py:20
  81.4 6.5 %psum.14 = f32[16]{0:T(128)S(1)} all-reduce(f32[16]{0:T(128)S(1)} %convert_reduce_fusion), channel_id=1, replica_groups=mesh['fsdp'=8,'dp'=4] {'dp'}, use_global_device_ids=true, to_apply=%region_1.0 | all-reduce | flops 16 | bytes 128 | tf_op jit(solution)/shard_map/psum | solution.py:26
  87.8 0.1 broadcast_in_dim.25
  87.9 0.1 broadcast_in_dim.26
  88.0 0.0 copy-done.3
  88.0 0.1 broadcast_in_dim.28
  88.1 0.1 sub.28
  88.2 0.1 broadcast_in_dim.29
  88.3 0.1 sub.30
  88.4 159.7 %all-reduce.2.cloned.1.call-done = f32[512,5120]{1,0:T(8,128)} async-done(((f32[512,5120]{1,0:T(8,128)}), f32[512,5120]{1,0:T(8,128)}) %all-reduce.2.cloned.1.call-update) | async-done | bytes 10485776 | tf_op jit(solution)/shard_map/psum | solution.py:26
  248.1 25.9 %fusion.3 = (bf16[512,5120]{1,0:T(8,128)(2,1)S(1)}, f32[512,5120]{1,0:T(8,128)}, f32[512,5120]{1,0:T(8,128)}, f32[512,5120]{1,0:T(8,128)}) fusion(f32[512,5120]{1,0:T(8,128)} %param.10, f32[5120]{0:T(1024)S(1)} %sub.30, f32[512,5120]{1,0:T(8,128)} %all-reduce.2.cloned.1.call-done, f32[512,5120]{1,0:T(8,128)} %param.12, f32[5120]{0:T(1024)S(1)} %sub.28, ...), kind=kLoop, calls=%fused_computation.13 | loop fusion | flops 44564480 | bytes 78689280 | tf_op jit(solution)/shard_map/convert_element_type | solution.py:38
  274.0 0.0 copy-start.1
  274.0 2.4 copy-done.1
  276.3 3.1 fusion.5
  279.4 0.0 reduce-scatter.2.cloned.1.call-update
  279.4 0.5 convert_add_fusion
  279.9 70.9 %reduce-scatter.2.cloned.1.call-done = f32[640,128]{1,0:T(8,128)} async-done(((f32[5120,128]{1,0:T(8,128)}), f32[640,128]{1,0:T(8,128)}) %reduce-scatter.2.cloned.1.call-update) | async-done | bytes 327696 | tf_op jit(solution)/shard_map/reduce_scatter | solution.py:40
  350.8 1.0 convert_bitcast_fusion
  351.8 0.8 copy.15
  (4 shorter events, 0.1 us)
Async XLA Ops:
  7.2 48.4 %copy-start = (bf16[128,512]{1,0:T(8,128)(2,1)S(1)}, bf16[128,512]{1,0:T(8,128)(2,1)}, u32[]{:S(2)}) copy-start(bf16[128,512]{1,0:T(8,128)(2,1)} %param.8) | copy-start | bytes 393220
  7.2 48.3 %all-gather.3.cloned.1.call-start = ((), (), s32[]{:S(2)}) async-start(), calls=%async_computation.1 | async-start | bytes 1474560 | tf_op jit(solution)/shard_map/all_gather | solution.py:19
  7.9 55.3 %copy-start.2 = (s32[1,16]{1,0:T(1,128)S(1)}, s32[1,16]{1,0:T(1,128)}, u32[]{:S(2)}) copy-start(s32[1,16]{1,0:T(1,128)} %param.13) | copy-start | bytes 196
  7.9 80.1 %copy-start.3 = (s32[16]{0:T(128)S(1)}, s32[16]{0:T(128)}, u32[]{:S(2)}) copy-start(s32[16]{0:T(128)} %param.14) | copy-start | bytes 196
  7.9 240.2 %all-reduce.2.cloned.1.call-start = ((), (), s32[]{:S(2)}) async-start(), calls=%async_computation.2 | async-start | bytes 20971520 | tf_op jit(solution)/shard_map/psum | solution.py:26
  62.5 288.3 %reduce-scatter.2.cloned.1.call-start = ((), (), s32[]{:S(2)}) async-start(), calls=%async_computation.3 | async-start | bytes 2949120 | tf_op jit(solution)/shard_map/reduce_scatter | solution.py:40
  274.0 2.4 copy-start.1
Sparse Core Ops, SparseCore 0:
  10.2 45.2 all-gather.2
  62.6 185.4 all-reduce.1
  279.5 71.2 reduce-scatter.1
where the time goes:
time: 359 us
  waiting for transfers between devices  279 us (78%)
  other arithmetic  27.4 us (8%)
  blocking collectives  24.6 us (7%)
  between operations  14.5 us (4%)
  matrix products  10 us (3%)
  local copies, waits for them, and re-layouts  3.66 us (1%)
    psum x1, waiting for transfers between devices, local(): gradient, counts = lax.psum((partial_value, local_counts), 'dp')  160 us
    reduce_scatter x1, waiting for transfers between devices, local(): lax.psum_scatter(lax.dot_general(weight_half, tokens, (((0,), (1,)), ((),...  70.9 us
    all_gather x1, waiting for transfers between devices, local(): lax.all_gather(out_grad, 'fsdp', axis=1, tiled=True)  47.5 us
    convert_element_type x1, other arithmetic, local(): weight_half = master_next.astype(jnp.bfloat16)  25.9 us
    all_gather x1, blocking collectives, local(): lax.all_gather(flags.astype(jnp.bfloat16), 'fsdp', axis=0, tiled=True)  18.1 us
  transfers between devices with their start and end apart: 3, of which 3 were waited for; matrix products, arithmetic and copies ran while one was open for 0% of the time, Pallas kernels for 0%

commit v1 on v0

--- a/solution.py
+++ b/solution.py
@@ -15,16 +15,15 @@
     width_out = master.shape[1]
     bucket_width = width_out // BUCKETS
     contract_rows = (((0,), (0,)), ((), ()))
-    gathered, flag_rows = (
-        lax.all_gather(out_grad, "fsdp", axis=1, tiled=True),
-        lax.all_gather(flags.astype(jnp.bfloat16), "fsdp", axis=0, tiled=True),
+    rows = lax.all_gather(tokens, "dp", axis=0, tiled=True)
+    grads = lax.all_gather(
+        lax.all_gather(out_grad, "fsdp", axis=1, tiled=True), "dp", axis=0, tiled=True
     )
-    partial_value = lax.dot_general(
-        tokens, gathered, contract_rows, preferred_element_type=jnp.float32
+    counts = lax.psum(flags[0], ("fsdp", "dp"))
+    gradient = lax.dot_general(
+        rows, grads, contract_rows, preferred_element_type=jnp.float32
     )
-    local_counts = jnp.sum(flag_rows.astype(jnp.float32), axis=0)
-    gradient, counts = lax.psum((partial_value, local_counts), "dp")
-    commit_bucket = counts == 0.0
+    commit_bucket = counts == 0
     commit = jnp.repeat(commit_bucket, bucket_width)[None, :]
     times = jnp.repeat(steps + 1, bucket_width).astype(jnp.float32)[None, :]
     first = first_decay * moment_one + (1.0 - first_decay) * gradient
@@ -37,14 +36,14 @@
     moment_two_next = jnp.where(commit, second, moment_two)
     weight_half = master_next.astype(jnp.bfloat16)
     steps_next = steps + commit_bucket.astype(jnp.int32)
-    result = lax.psum_scatter(
-        lax.dot_general(
-            weight_half, tokens, (((0,), (1,)), ((), ())), preferred_element_type=jnp.float32
-        ),
-        "fsdp",
-        scatter_dimension=0,
-        tiled=True,
-    ).T
+    share = lax.dot_general(
+        tokens, weight_half, (((1,), (0,)), ((), ())), preferred_element_type=jnp.float32
+    ).astype(jnp.bfloat16)
+    shards = lax.axis_size("fsdp")
+    pieces = share.reshape(share.shape[0], shards, -1).transpose(1, 0, 2)
+    result = jnp.sum(
+        lax.all_to_all(pieces, "fsdp", 0, 0).astype(jnp.float32), axis=0
+    )
     return (
         master_next,
         moment_one_next,

time: 359 us -> 181 us (0.50)
  waiting for transfers between devices: 279 us -> 79.6 us
  other arithmetic: 27.4 us -> 1.4 us
  blocking collectives: 24.6 us -> 47.8 us
  matrix products: 10 us -> 31.7 us
  starting transfers between devices: 0.12 us -> 3.94 us
    psum x1 -> x0, waiting for transfers between devices: 160 us -> none  [local(): gradient, counts = lax.psum((partial_value, local_counts), 'dp')]
    reduce_scatter x1 -> x0, waiting for transfers between devices: 70.9 us -> none  [local(): lax.psum_scatter(lax.dot_general(weight_half, tokens, (((0,), (1,)), ((),...]
    psum x1, blocking collectives: 6.48 us -> 39.6 us  [local(): counts = lax.psum(flags[0], ('fsdp', 'dp'))]
    all_to_all x0 -> x1, waiting for transfers between devices: none -> 31.4 us  [local(): lax.all_to_all(pieces, 'fsdp', 0, 0).astype(jnp.float32)]
    convert_element_type x2 -> x0, other arithmetic: 26.9 us -> none  [the longest x1 25.9 us: local(): weight_half = master_next.astype(jnp.bfloat16)]
    dot_general x2, matrix products: 10 us -> 31.7 us  [the longest x1 26.5 us: local(): lax.dot_general(rows, grads, contract_rows, preferred_element_type=jnp.fl...]
    all_gather x1, blocking collectives: 18.1 us -> 8.16 us  [local(): rows = lax.all_gather(tokens, 'dp', axis=0, tiled=True)]
    all_to_all x0 -> x1, starting transfers between devices: none -> 3.87 us  [local(): lax.all_to_all(pieces, 'fsdp', 0, 0).astype(jnp.float32)]
  transfers between devices with their start and end apart: 3 -> 3, of which waited for: 3 -> 2; matrix products, arithmetic and copies ran while one was open for 0% -> 1% of each run, Pallas kernels for 0% -> 0%
where the time goes in v1:
time: 181 us; the launch traced here: 180 us
  waiting for transfers between devices  79.6 us (44%)
  blocking collectives  47.8 us (26%)
  matrix products  31.7 us (18%)
  between operations  14.7 us (8%)
  starting transfers between devices  3.94 us (2%)
    all_gather x1, waiting for transfers between devices, local(): lax.all_gather(out_grad, 'fsdp', axis=1, tiled=True)  47.6 us
    psum x1, blocking collectives, local(): counts = lax.psum(flags[0], ('fsdp', 'dp'))  39.6 us
    all_to_all x1, waiting for transfers between devices, local(): lax.all_to_all(pieces, 'fsdp', 0, 0).astype(jnp.float32)  31.4 us
    dot_general x1, matrix products, local(): lax.dot_general(rows, grads, contract_rows, preferred_element_type=jnp.fl...  26.5 us
    all_gather x1, blocking collectives, local(): rows = lax.all_gather(tokens, 'dp', axis=0, tiled=True)  8.16 us
    dot_general x1, matrix products, local(): lax.dot_general(tokens, weight_half, (((1,), (0,)), ((), ())), preferred_...  5.16 us
    all_to_all x1, starting transfers between devices, local(): lax.all_to_all(pieces, 'fsdp', 0, 0).astype(jnp.float32)  3.87 us
  transfers between devices with their start and end apart: 3, of which 2 were waited for; matrix products, arithmetic and copies ran while one was open for 1% of the time, Pallas kernels for 0%

profile of v1, /device:TPU:0, one launch (start us, length us, event | category | flops | bytes accessed | tf_op | source)
XLA Modules:
  0.0 180.5 jit_solution(914096782585376441)
XLA Ops:
  7.2 0.0 all-gather.3.cloned.1.call-start
  7.2 0.7 all-gather.3.cloned.1.call-update
  7.9 0.0 all-gather.5.cloned.1.call-start
  7.9 47.6 %all-gather.3.cloned.1.call-done = bf16[128,5120]{1,0:T(8,128)(2,1)} async-done(((bf16[128,640]{1,0:T(8,128)(2,1)}), bf16[128,5120]{1,0:T(8,128)(2,1)}) %all-gather.3.cloned.1.call-update) | async-done | bytes 1310736 | tf_op jit(solution)/shard_map/all_gather | solution.py:20
  55.5 0.0 all-gather.5.cloned.1.call-update
  55.5 39.6 %psum.7 = s32[16]{0:T(128)S(1)} all-reduce(s32[16]{0:T(128)} %bitcast.12), channel_id=1, replica_groups=mesh['fsdp'=8,'dp'=4] {'fsdp','dp'}, use_global_device_ids=true, to_apply=%region_0.0 | all-reduce | flops 16 | bytes 128 | tf_op jit(solution)/shard_map/psum | solution.py:22
  95.9 0.1 broadcast_in_dim.25
  95.9 0.1 broadcast_in_dim.26
  96.0 0.7 power_subtract_fusion.1
  96.7 0.1 broadcast_in_dim.28
  96.8 0.1 sub.28
  96.8 0.1 broadcast_in_dim.29
  96.9 0.1 sub.30
  97.0 8.2 %all_gather.9 = bf16[512,512]{1,0:T(8,128)(2,1)S(1)} all-gather(bf16[128,512]{1,0:T(8,128)(2,1)} %param.8), channel_id=1, replica_groups=mesh['fsdp'=8,'dp'=4] {'dp'}, dimensions={0}, use_global_device_ids=true | all-gather | bytes 655360 | tf_op jit(solution)/shard_map/all_gather | solution.py:18
  105.2 0.0 all-gather.5.cloned.1.call-done
  105.2 0.0 copy-start
  105.2 0.0 copy-start.1
  105.2 26.5 %fusion.3 = (bf16[512,5120]{1,0:T(8,128)(2,1)}, f32[512,5120]{1,0:T(8,128)}, f32[512,5120]{1,0:T(8,128)}, f32[512,5120]{1,0:T(8,128)}) fusion(f32[512,5120]{1,0:T(8,128)} %param.10, f32[5120]{0:T(1024)S(1)} %sub.30, f32[512,5120]{1,0:T(8,128)} %param.12, f32[5120]{0:T(1024)S(1)} %sub.28, f32[512,5120]{1,0:T(8,128)} %param.11, f32[]{:T(128)} %bitcast.11, ...), kind=kOutput, calls=%fused_computation.11 | convolution fusion | flops 2728919040 | bytes 73970688 | tf_op jit(solution)/shard_map/dot_general | solution.py:23
  131.7 0.0 copy-done
  131.7 5.2 %convolution_convert_fusion = bf16[5120,128]{1,0:T(8,128)(2,1)} fusion(bf16[512,5120]{1,0:T(8,128)(2,1)} %get-tuple-element.12, bf16[128,512]{1,0:T(8,128)(2,1)S(1)} %copy-done), kind=kOutput, calls=%fused_computation.6 | convolution fusion | flops 671744000 | bytes 6684672 | tf_op jit(solution)/shard_map/dot_general | solution.py:39
  136.8 3.9 %all-to-all-start = ((bf16[8,128,640]{1,2,0:T(8,128)(2,1)}), bf16[8,128,640]{1,2,0:T(8,128)(2,1)S(1)}, u32[]{:S(2)}, u32[]{:S(2)}) async-start(bf16[8,128,640]{1,2,0:T(8,128)(2,1)} %bitcast.4), calls=%async_computation | async-start | bytes 2621440 | tf_op jit(solution)/shard_map/all_to_all | solution.py:45
  140.7 0.0 copy-done.1
  140.7 0.5 convert_add_fusion
  141.2 31.4 %all-to-all-done = bf16[8,128,640]{1,2,0:T(8,128)(2,1)S(1)} async-done(((bf16[8,128,640]{1,2,0:T(8,128)(2,1)}), bf16[8,128,640]{1,2,0:T(8,128)(2,1)S(1)}, u32[]{:S(2)}, u32[]{:S(2)}) %all-to-all-start) | async-done | bytes 1310752 | tf_op jit(solution)/shard_map/all_to_all | solution.py:45
  172.6 0.2 reduce_sum.12
  172.8 0.8 copy.14
  (1 shorter events, 0.0 us)
Async XLA Ops:
  7.2 48.3 %all-gather.3.cloned.1.call-start = ((), (), s32[]{:S(2)}) async-start(), calls=%async_computation.1 | async-start | bytes 1474560 | tf_op jit(solution)/shard_map/all_gather | solution.py:20
  7.9 97.3 %all-gather.5.cloned.1.call-start = ((), (), s32[]{:S(2)}) async-start(), calls=%async_computation.2 | async-start | bytes 6553600 | tf_op jit(solution)/shard_map/all_gather | solution.py:19
  105.2 26.5 %copy-start = (bf16[128,512]{1,0:T(8,128)(2,1)S(1)}, bf16[128,512]{1,0:T(8,128)(2,1)}, u32[]{:S(2)}) copy-start(bf16[128,512]{1,0:T(8,128)(2,1)} %param.8) | copy-start | bytes 393220
  105.2 35.6 %copy-start.1 = (s32[16]{0:T(128)S(1)}, s32[16]{0:T(128)}, u32[]{:S(2)}) copy-start(s32[16]{0:T(128)} %param.14) | copy-start | bytes 196
  136.8 35.8 %all-to-all-start = ((bf16[8,128,640]{1,2,0:T(8,128)(2,1)}), bf16[8,128,640]{1,2,0:T(8,128)(2,1)S(1)}, u32[]{:S(2)}, u32[]{:S(2)}) async-start(bf16[8,128,640]{1,2,0:T(8,128)(2,1)} %bitcast.4), calls=%async_computation | async-start | bytes 2621440 | tf_op jit(solution)/shard_map/all_to_all | solution.py:45
Sparse Core Ops, SparseCore 0:
  10.2 45.2 all-gather.2
  57.1 39.8 all-gather.4

commit v2 on v1

--- a/solution.py
+++ b/solution.py
@@ -1,6 +1,10 @@
+import functools
+
 import jax
 import jax.numpy as jnp
 from jax import lax
+from jax.experimental import pallas as pl
+from jax.experimental.pallas import tpu as pltpu
 from jax.sharding import PartitionSpec as P
 
 BUCKETS = 16
@@ -11,7 +15,7 @@
 epsilon = 1e-08
 
 
-def local(tokens, out_grad, master, moment_one, moment_two, flags, steps, rate):
+def plain(tokens, out_grad, master, moment_one, moment_two, flags, steps, rate):
     width_out = master.shape[1]
     bucket_width = width_out // BUCKETS
     contract_rows = (((0,), (0,)), ((), ()))
@@ -54,6 +58,287 @@
     )
 
 
+def exchange(
+    nf, bucket_width,
+    tok, tokt, og, flag, coef, master, one, two,
+    master_o, one_o, two_o, half_o, count_o, out_o,
+    obuf, tbuf, grad, commit, fl, ysend, yrecv, zsend, zrecv, acc,
+    read_sem, loc_sem,
+    fz_s, fz_r, f_s, f_r, t_s, t_r,
+    z_s, z_r, y_s, y_r, x_s, x_r, c_s, c_r, d_s, d_r, ry_s, ry_r, rz_s, rz_r,
+):
+    nz = nf // 2
+    f, d = lax.axis_index("fsdp"), lax.axis_index("dp")
+    yp = f + 1 - 2 * lax.rem(f, 2)
+    sib, xn = d + 1 - 2 * lax.rem(d, 2), lax.rem(d + 2, 4)
+    toks, width = og.shape
+    rows = tok.shape[1]
+
+    def peer(k):
+        return lax.rem(f + 2 * k, nf)
+
+    def column(par, k):
+        return lax.rem(f + par * (1 - 2 * lax.rem(f, 2)) + 2 * k, nf)
+
+    def span(block):
+        return pl.ds(pl.multiple_of(block * width, 128), width)
+
+    def slot(dd):
+        return pl.ds(pl.multiple_of(dd * toks, 128), toks)
+
+    def piece(block, dd):
+        return obuf.at[block, slot(dd)]
+
+    def send(src, dst, ssem, rsem, ff, dd):
+        return pltpu.make_async_remote_copy(
+            src_ref=src, dst_ref=dst, send_sem=ssem, recv_sem=rsem,
+            device_id={"fsdp": ff, "dp": dd}, device_id_type=pl.DeviceIdType.MESH,
+        )
+
+    def z_copy(k):
+        return send(og, piece(f, d), z_s.at[k], z_r.at[nz - k], peer(k), d)
+
+    def y_copy(k):
+        p = piece(column(0, k), d)
+        return send(p, p, y_s.at[k], y_r.at[k], yp, d)
+
+    def x_copy(par, k):
+        p, j = piece(column(par, k), d), par * nz + k
+        return send(p, p, x_s.at[j], x_r.at[j], f, xn)
+
+    def c_copy(par, k):
+        p, j = piece(column(par, k), d), par * nz + k
+        return send(p, p, c_s.at[j], c_r.at[j], f, sib)
+
+    def d_copy(par, k):
+        p, j = piece(column(par, k), xn), par * nz + k
+        return send(p, p, d_s.at[j], d_r.at[j], f, sib)
+
+    def t_copy(i):
+        p = tbuf.at[:, slot(xn if i == 2 else d)]
+        return send(p if i == 2 else tokt, p, t_s.at[i], t_r.at[i], f, xn if i == 0 else sib)
+
+    def fz_copy(k):
+        return send(flag, fl.at[nz - k], fz_s.at[k], fz_r.at[nz - k], peer(k), d)
+
+    def f_copy(i):
+        n = nz << i
+        ff, dd = ((yp, d), (f, xn), (f, sib))[i]
+        return send(fl.at[pl.ds(0, n)], fl.at[pl.ds(n, n)], f_s.at[i], f_r.at[i], ff, dd)
+
+    def ry_copy(k):
+        return send(ysend.at[k], yrecv.at[k], ry_s.at[k], ry_r.at[k], yp, d)
+
+    def rz_copy(k):
+        return send(zsend.at[k], zrecv.at[nz - k], rz_s.at[k], rz_r.at[nz - k], peer(k), d)
+
+    state = ((master, master_o), (one, one_o), (two, two_o))
+
+    def read(i, par, k):
+        cols = span(column(par, k))
+        return pltpu.make_async_copy(
+            state[i][0].at[:, cols], state[i][1].at[:, cols], read_sem.at[i, par * nz + k]
+        )
+
+    @pl.loop(0, nz)
+    def _(k):
+        for par in (1, 0):
+            for i in range(3):
+                read(i, par, k).start()
+
+    own = (
+        pltpu.make_async_copy(og, piece(f, d), loc_sem.at[0]),
+        pltpu.make_async_copy(tokt, tbuf.at[:, slot(d)], loc_sem.at[1]),
+        pltpu.make_async_copy(flag, fl.at[0], loc_sem.at[2]),
+    )
+    for copy in own:
+        copy.start()
+
+    barrier = pltpu.get_barrier_semaphore()
+    near = [(peer(k), d) for k in range(1, nz)] + [(yp, d), (f, xn), (f, sib)]
+    for ff, dd in near:
+        pl.semaphore_signal(
+            barrier, inc=1, device_id={"fsdp": ff, "dp": dd},
+            device_id_type=pl.DeviceIdType.MESH,
+        )
+    pl.semaphore_wait(barrier, len(near))
+
+    for k in range(1, nz):
+        fz_copy(k).start()
+    t_copy(0).start()
+    t_copy(1).start()
+    for k in range(1, nz):
+        z_copy(k).start()
+    for copy in own:
+        copy.wait()
+    y_copy(0).start()
+    x_copy(0, 0).start()
+    c_copy(0, 0).start()
+    for k in range(1, nz):
+        fz_copy(k).wait_send()
+        fz_copy(nz - k).wait_recv()
+    f_copy(0).start()
+    y_copy(0).wait_recv()
+    x_copy(1, 0).start()
+    c_copy(1, 0).start()
+    f_copy(0).wait()
+    f_copy(1).start()
+    t_copy(0).wait()
+    t_copy(2).start()
+    f_copy(1).wait()
+    f_copy(2).start()
+    t_copy(1).wait()
+    t_copy(2).wait()
+    f_copy(2).wait()
+
+    counts = jnp.sum(fl[...], axis=0)
+    count_o[...] = counts
+    buckets = commit.shape[1] // bucket_width
+    where = lax.broadcasted_iota(jnp.int32, commit.shape, 1) // bucket_width
+    ok = jnp.zeros(commit.shape, jnp.int32)
+    for b in range(buckets):
+        ok = jnp.where(where == b, counts[:, b : b + 1], ok)
+    commit[...] = ok
+
+    @pl.loop(0, 2 * nz)
+    def _(step):
+        k = step // 2
+        par = 1 - lax.rem(step, 2)
+
+        @pl.when((par == 1) & (k + 1 < nz))
+        def _():
+            n = k + 1
+            send(og, piece(f, d), z_s.at[n], z_r.at[n], peer(n), d).wait_recv()
+            y_copy(n).start()
+            y_copy(n).wait_recv()
+            for q in (1, 0):
+                x_copy(q, n).start()
+                c_copy(q, n).start()
+
+        x_copy(par, k).wait_recv()
+        d_copy(par, k).start()
+        c_copy(par, k).wait_recv()
+        d_copy(par, k).wait_recv()
+        for i in range(3):
+            read(i, par, k).wait()
+        block = column(par, k)
+        cols = span(block)
+        grad[...] = jnp.dot(tbuf[...], obuf[block], preferred_element_type=jnp.float32)
+        scale_one = coef[0:1, cols]
+        scale_two = coef[1:2, cols]
+        keep = commit[0:1, cols] == 0
+
+        @pl.loop(0, rows // 16)
+        def _(r):
+            lines = pl.ds(pl.multiple_of(r * 16, 16), 16)
+            g = grad[lines, :]
+            old = master_o[lines, cols]
+            old_one = one_o[lines, cols]
+            old_two = two_o[lines, cols]
+            first = first_decay * old_one + (1.0 - first_decay) * g
+            second = second_decay * old_two + (1.0 - second_decay) * g * g
+            new = old - (first * scale_one) / (jnp.sqrt(second * scale_two) + epsilon)
+            new = jnp.where(keep, new, old)
+            master_o[lines, cols] = new
+            half_o[lines, cols] = new.astype(jnp.bfloat16)
+            one_o[lines, cols] = jnp.where(keep, first, old_one)
+            two_o[lines, cols] = jnp.where(keep, second, old_two)
+
+        share = jnp.dot(tok[...], half_o[:, cols], preferred_element_type=jnp.float32)
+
+        @pl.when(par == 1)
+        def _():
+            ysend[k] = share.astype(jnp.bfloat16)
+            ry_copy(k).start()
+
+        @pl.when(par == 0)
+        def _():
+            ry_copy(k).wait_recv()
+            both = share + yrecv[k].astype(jnp.float32)
+
+            @pl.when(k == 0)
+            def _():
+                acc[...] = both
+
+            @pl.when(k > 0)
+            def _():
+                zsend[k] = both.astype(jnp.bfloat16)
+                rz_copy(k).start()
+
+    total = acc[...]
+    for k in range(1, nz):
+        rz_copy(nz - k).wait_recv()
+        total = total + zrecv[k].astype(jnp.float32)
+    out_o[...] = total.astype(jnp.bfloat16)
+
+    for k in range(nz):
+        y_copy(k).wait_send()
+        ry_copy(k).wait_send()
+        if k > 0:
+            z_copy(k).wait_send()
+            rz_copy(k).wait_send()
+        for par in (0, 1):
+            x_copy(par, k).wait_send()
+            c_copy(par, k).wait_send()
+            d_copy(par, k).wait_send()
+
+
+def local(tokens, out_grad, master, moment_one, moment_two, flags, steps, rate):
+    nf, nd = lax.axis_size("fsdp"), lax.axis_size("dp")
+    toks, width = out_grad.shape
+    rows, columns = master.shape
+    nz = nf // 2
+    if width % 128 or toks % 128 or rows % 128 or nd != 4 or nf % 2 or nf < 4:
+        return plain(
+            tokens, out_grad, master, moment_one, moment_two, flags, steps, rate
+        )
+    bucket_width = columns // BUCKETS
+    times = (steps + 1).astype(jnp.float32)
+    one = rate[0] / (1.0 - jnp.power(jnp.float32(first_decay), times))
+    two = 1.0 / (1.0 - jnp.power(jnp.float32(second_decay), times))
+    coef = jnp.repeat(jnp.stack([one, two]), bucket_width, axis=1)
+    flag = jnp.pad(flags, ((0, 7), (0, 128 - BUCKETS)))
+    vmem = pl.BlockSpec(memory_space=pltpu.VMEM)
+    anyw = pl.BlockSpec(memory_space=pl.ANY)
+    full = (rows, columns)
+    bf, f32, dma = jnp.bfloat16, jnp.float32, pltpu.SemaphoreType.DMA
+    pairs = lambda n: [dma((n,)), dma((n,))]
+    master_n, one_n, two_n, half, counts, outputs = pl.pallas_call(
+        functools.partial(exchange, nf, bucket_width),
+        out_shape=(
+            pltpu.VMEM(full, f32),
+            pltpu.VMEM(full, f32),
+            pltpu.VMEM(full, f32),
+            jax.ShapeDtypeStruct(full, bf),
+            jax.ShapeDtypeStruct((8, 128), jnp.int32),
+            jax.ShapeDtypeStruct((toks, width), bf),
+        ),
+        in_specs=[vmem] * 5 + [anyw] * 3,
+        out_specs=[vmem] * 6,
+        scratch_shapes=[
+            pltpu.VMEM((nf, nd * toks, width), bf),
+            pltpu.VMEM((rows, nd * toks), bf),
+            pltpu.VMEM((rows, width), f32),
+            pltpu.VMEM((8, columns), jnp.int32),
+            pltpu.VMEM((8 * nz, 8, 128), jnp.int32),
+            pltpu.VMEM((nz, toks, width), bf),
+            pltpu.VMEM((nz, toks, width), bf),
+            pltpu.VMEM((nz, toks, width), bf),
+            pltpu.VMEM((nz, toks, width), bf),
+            pltpu.VMEM((toks, width), f32),
+            dma((3, nf)),
+            dma((3,)),
+        ]
+        + pairs(nz) + pairs(3) + pairs(3)
+        + pairs(nz) + pairs(nz) + pairs(nf) + pairs(nf) + pairs(nf) + pairs(nz) + pairs(nz),
+        compiler_params=pltpu.CompilerParams(
+            collective_id=0, has_side_effects=True, vmem_limit_bytes=24000000
+        ),
+    )(tokens, tokens.T, out_grad, flag, coef, master, moment_one, moment_two)
+    steps_next = steps + (counts[0, :BUCKETS] == 0).astype(jnp.int32)
+    return master_n, one_n, two_n, half, steps_next, outputs
+
+
 def solution(mesh):
     in_specs = (
         P("dp", "fsdp"),

time: 181 us -> 108 us (0.60)
  Pallas kernels: 0 us -> 83.8 us
  waiting for transfers between devices: 79.6 us -> 0 us
  blocking collectives: 47.8 us -> 0 us
  matrix products: 31.7 us -> 0 us
  local copies, waits for them, and re-layouts: 1.29 us -> 21.1 us
  between operations: 14.7 us -> 1.32 us
  starting transfers between devices: 3.94 us -> 0 us
    pallas_call x0 -> x1, Pallas kernels: none -> 83.8 us  [local(): pl.pallas_call(functools.partial(exchange, nf, bucket_width), out_shape=(...]
    all_gather x2 -> x0, waiting for transfers between devices: 47.6 us -> none  [the longest x1 47.6 us: local(): lax.all_gather(out_grad, 'fsdp', axis=1, tiled=True)]
    psum x1 -> x0, blocking collectives: 39.6 us -> none  [local(): counts = lax.psum(flags[0], ('fsdp', 'dp'))]
    dot_general x2 -> x0, matrix products: 31.7 us -> none  [the longest x1 26.5 us: local(): lax.dot_general(rows, grads, contract_rows, preferred_element_type=jnp.fl...]
    all_to_all x1 -> x0, waiting for transfers between devices: 31.4 us -> none  [local(): lax.all_to_all(pieces, 'fsdp', 0, 0).astype(jnp.float32)]
    unnamed x5 -> x14, local copies, waits for them, and re-layouts: 0.82 us -> 20.3 us
    all_gather x1 -> x0, blocking collectives: 8.16 us -> none  [local(): rows = lax.all_gather(tokens, 'dp', axis=0, tiled=True)]
    all_to_all x1 -> x0, starting transfers between devices: 3.87 us -> none  [local(): lax.all_to_all(pieces, 'fsdp', 0, 0).astype(jnp.float32)]
  transfers between devices with their start and end apart: 3 -> 0, of which waited for: 2 -> 0; matrix products, arithmetic and copies ran while one was open for 1% -> 0% of each run, Pallas kernels for 0% -> 0%
where the time goes in v2:
time: 108 us; the launch traced here: 107 us
  Pallas kernels  83.8 us (78%)
  local copies, waits for them, and re-layouts  21.1 us (20%)
  between operations  1.32 us (1%)
  other arithmetic  1.19 us (1%)
    pallas_call x1, Pallas kernels, local(): pl.pallas_call(functools.partial(exchange, nf, bucket_width), out_shape=(...  83.8 us
    unnamed x14, local copies, waits for them, and re-layouts  20.3 us

profile of v2, /device:TPU:0, one launch (start us, length us, event | category | flops | bytes accessed | tf_op | source)
XLA Modules:
  0.0 107.5 jit_solution(1810604775809506406)
XLA Ops:
  1.3 0.7 divide_bitcast_fusion.1
  2.0 0.7 pad.4.flag
  2.6 0.1 broadcast_in_dim.3
  2.7 0.1 reshape.19.coef
  2.8 1.0 copy.14
  3.8 0.0 copy-start
  3.8 0.9 copy-done
  4.7 0.0 copy-start.1
  4.7 0.9 copy-done.1
  5.7 83.8 %shard_map.127 = (f32[512,5120]{1,0:T(8,128)S(1)}, f32[512,5120]{1,0:T(8,128)S(1)}, f32[512,5120]{1,0:T(8,128)S(1)}, bf16[512,5120]{1,0:T(8,128)(2,1)}, s32[8,12...) custom-call(bf16[128,512]{1,0:T(8,128)(2,1)S(1)} %copy-done, bf16[512,128]{1,0:T(8,128)(2,1)S(1)} %bitcast.11, ...), custom_call_target="tpu_custom_call" | custom-call | tf_op jit(solution)/shard_map/pallas_call | solution.py:306
  89.5 0.0 copy-start.3
  89.5 4.1 %copy.20 = f32[512,5120]{1,0:T(8,128)} copy(f32[512,5120]{1,0:T(8,128)S(1)} %get-tuple-element.20) | data formatting | bytes 20971520
  93.6 0.0 copy-done.3
  93.6 0.5 fusion.1
  94.1 4.1 %copy.21 = f32[512,5120]{1,0:T(8,128)} copy(f32[512,5120]{1,0:T(8,128)S(1)} %get-tuple-element.21) | data formatting | bytes 20971520
  98.2 0.0 copy-start.2
  98.2 5.3 %copy.22 = f32[512,5120]{1,0:T(8,128)} copy(f32[512,5120]{1,0:T(8,128)S(1)} %get-tuple-element.22) | data formatting | bytes 20971520
  103.5 1.0 copy-done.2
  104.5 2.4 %copy.24 = bf16[512,5120]{1,0:T(8,128)(2,1)} copy(bf16[512,5120]{1,0:T(8,128)(2,1)S(1)} %copy-done.2) | data formatting | bytes 10485760
  106.8 0.7 copy.25
  (1 shorter events, 0.0 us)
Async XLA Ops:
  3.8 0.9 copy-start
  4.7 0.9 copy-start.1
  89.5 4.1 %copy-start.3 = (s32[16]{0:T(128)S(1)}, s32[16]{0:T(128)}, u32[]{:S(2)}) copy-start(s32[16]{0:T(128)} %param.14) | copy-start | bytes 196
  98.2 6.3 %copy-start.2 = (bf16[512,5120]{1,0:T(8,128)(2,1)S(1)}, bf16[512,5120]{1,0:T(8,128)(2,1)}, u32[]{:S(2)}) copy-start(bf16[512,5120]{1,0:T(8,128)(2,1)} %get-tuple-element.35) | copy-start | bytes 15728644

commit v3 on v2

--- a/solution.py
+++ b/solution.py
@@ -228,16 +228,17 @@
         scale_two = coef[1:2, cols]
         keep = commit[0:1, cols] == 0
 
-        @pl.loop(0, rows // 16)
+        @pl.loop(0, rows // 64, unroll=1)
         def _(r):
-            lines = pl.ds(pl.multiple_of(r * 16, 16), 16)
+            lines = pl.ds(pl.multiple_of(r * 64, 64), 64)
             g = grad[lines, :]
             old = master_o[lines, cols]
             old_one = one_o[lines, cols]
             old_two = two_o[lines, cols]
             first = first_decay * old_one + (1.0 - first_decay) * g
             second = second_decay * old_two + (1.0 - second_decay) * g * g
-            new = old - (first * scale_one) / (jnp.sqrt(second * scale_two) + epsilon)
+            fixed = second * scale_two
+            new = old - (first * scale_one) / (fixed * lax.rsqrt(fixed) + epsilon)
             new = jnp.where(keep, new, old)
             master_o[lines, cols] = new
             half_o[lines, cols] = new.astype(jnp.bfloat16)

time: 108 us -> 106 us (0.981)
  Pallas kernels: 83.8 us -> 81.9 us
    pallas_call x1, Pallas kernels: 83.8 us -> 81.9 us  [local(): pl.pallas_call(functools.partial(exchange, nf, bucket_width), out_shape=(...]
where the time goes in v3:
time: 106 us
  Pallas kernels  81.9 us (77%)
  local copies, waits for them, and re-layouts  21.1 us (20%)
  between operations  1.32 us (1%)
  other arithmetic  1.19 us (1%)
    pallas_call x1, Pallas kernels, local(): pl.pallas_call(functools.partial(exchange, nf, bucket_width), out_shape=(...  81.9 us
    unnamed x14, local copies, waits for them, and re-layouts  20.3 us

profile of v3, /device:TPU:0, one launch (start us, length us, event | category | flops | bytes accessed | tf_op | source)
XLA Modules:
  0.0 105.5 jit_solution(7388256412344249051)
XLA Ops:
  1.3 0.7 divide_bitcast_fusion.1
  2.0 0.7 pad.4.flag
  2.6 0.1 broadcast_in_dim.3
  2.7 0.1 reshape.19.coef
  2.8 1.0 copy.14
  3.8 0.0 copy-start
  3.8 0.9 copy-done
  4.7 0.0 copy-start.1
  4.7 0.9 copy-done.1
  5.7 81.9 %shard_map.127 = (f32[512,5120]{1,0:T(8,128)S(1)}, f32[512,5120]{1,0:T(8,128)S(1)}, f32[512,5120]{1,0:T(8,128)S(1)}, bf16[512,5120]{1,0:T(8,128)(2,1)}, s32[8,12...) custom-call(bf16[128,512]{1,0:T(8,128)(2,1)S(1)} %copy-done, bf16[512,128]{1,0:T(8,128)(2,1)S(1)} %bitcast.11, ...), custom_call_target="tpu_custom_call" | custom-call | tf_op jit(solution)/shard_map/pallas_call | solution.py:307
  87.5 0.0 copy-start.3
  87.6 4.1 %copy.20 = f32[512,5120]{1,0:T(8,128)} copy(f32[512,5120]{1,0:T(8,128)S(1)} %get-tuple-element.20) | data formatting | bytes 20971520
  91.6 0.0 copy-done.3
  91.7 0.5 fusion.1
  92.2 4.1 %copy.21 = f32[512,5120]{1,0:T(8,128)} copy(f32[512,5120]{1,0:T(8,128)S(1)} %get-tuple-element.21) | data formatting | bytes 20971520
  96.3 0.0 copy-start.2
  96.3 5.3 %copy.22 = f32[512,5120]{1,0:T(8,128)} copy(f32[512,5120]{1,0:T(8,128)S(1)} %get-tuple-element.22) | data formatting | bytes 20971520
  101.6 1.0 copy-done.2
  102.5 2.4 %copy.24 = bf16[512,5120]{1,0:T(8,128)(2,1)} copy(bf16[512,5120]{1,0:T(8,128)(2,1)S(1)} %copy-done.2) | data formatting | bytes 10485760
  104.9 0.7 copy.25
  (1 shorter events, 0.0 us)
Async XLA Ops:
  3.8 0.9 copy-start
  4.7 0.9 copy-start.1
  87.5 4.1 %copy-start.3 = (s32[16]{0:T(128)S(1)}, s32[16]{0:T(128)}, u32[]{:S(2)}) copy-start(s32[16]{0:T(128)} %param.14) | copy-start | bytes 196
  96.3 6.3 %copy-start.2 = (bf16[512,5120]{1,0:T(8,128)(2,1)S(1)}, bf16[512,5120]{1,0:T(8,128)(2,1)}, u32[]{:S(2)}) copy-start(bf16[512,5120]{1,0:T(8,128)(2,1)} %get-tuple-element.35) | copy-start | bytes 15728644
